TPU v7x, 8 devices: a whole 2x2x1 slice. The times are simulated.
8 devices in a mesh: tp: 8 (over z, y, x, core).
Axes of the slice: x: 2, y: 2, z: 1, core: 2. Of those that a mesh axis runs over, the one named last changes fastest.
Arguments:
- x_norm: bfloat16 [8192, 1024], P(None, 'tp')
- hid_act: bfloat16 [8192, 2816], P(None, 'tp')
- dy_in: bfloat16 [2, 8192, 2816], replicated
- dy_out: bfloat16 [8192, 1024], replicated
- w_in: float32 [2, 1024, 2816], P(None, 'tp')
- w_out: float32 [2816, 1024], P('tp')
- row_in: float32 [2, 1024], P(None, 'tp')
- col_in: float32 [2, 2816], replicated
- row_out: float32 [2816], P('tp')
- col_out: float32 [1024], replicated
- beta_two: float32 [], replicated
- rel_step: float32 [], replicated
- clip_rms: float32 [], replicated
- clip_norm: float32 [], replicated
Outputs:
- output 1: float32 [2, 1024, 2816], P(None, 'tp')
- output 2: float32 [2, 1024], P(None, 'tp')
- output 3: float32 [2, 2816], replicated
- output 4: float32 [2816, 1024], P('tp')
- output 5: float32 [2816], P('tp')
- output 6: float32 [1024], replicated
All inputs are finite; a program needn't handle non-finite values.
Results may differ from a plain program's by a relative error of at most 0.001.
Values are sent between devices in bfloat16 or wider.
A program may use at most 1 GiB of HBM per device.

v0:
```python
import jax
import jax.numpy as jnp
from jax import lax
from jax.sharding import PartitionSpec as P

EPS_ONE = 1e-30
EPS_TWO = 1e-3


def local_sums(gradient, weight, row_stat):
    col_sq = jnp.sum(gradient * gradient, axis=-2)
    row_sum = jnp.sum(row_stat, axis=-1, keepdims=True)
    w_sq = jnp.sum(weight * weight, axis=(-2, -1))[..., None]
    return jnp.concatenate([col_sq, row_sum, w_sq], axis=-1)


def apply_update(weight, gradient, row_stat, col_stat, totals, shards, beta_two, rel_step, clip_rms, grad_scale):
    rows_total = gradient.shape[-2] * shards
    col_count = gradient.shape[-1]
    col_sq = totals[..., :-2]
    row_sum = totals[..., -2:-1]
    w_sq = totals[..., -1:]
    mix_new = 1.0 - beta_two
    sq_scale = grad_scale * grad_scale
    scaled = grad_scale * gradient
    sq_grad = scaled * scaled + EPS_ONE
    row_new = beta_two * row_stat + mix_new * jnp.mean(sq_grad, axis=-1)
    col_new = beta_two * col_stat + mix_new * (sq_scale * col_sq / rows_total + EPS_ONE)
    grand_sum = jnp.sum(col_sq, axis=-1, keepdims=True)
    row_level = beta_two * row_sum / rows_total + mix_new * (sq_scale * grand_sum / (rows_total * col_count) + EPS_ONE)
    second = (row_new / row_level)[..., :, None] * col_new[..., None, :]
    update = scaled / jnp.sqrt(second)
    upd_sq = lax.psum(jnp.sum(update * update, axis=(-2, -1)), 'tp')
    upd_rms = jnp.sqrt(upd_sq / (rows_total * col_count))[..., None, None]
    clipped = update / jnp.maximum(1.0, upd_rms / clip_rms)
    w_rms = jnp.sqrt(w_sq / (rows_total * col_count))[..., None]
    step_size = rel_step * jnp.maximum(EPS_TWO, w_rms)
    return (weight - step_size * clipped, row_new, col_new)


def solution(mesh):
    shards = mesh.shape['tp']

    def local_step(x_norm, hid_act, dy_in, dy_out, w_in, w_out, row_in, col_in, row_out, col_out, beta_two, rel_step, clip_rms, clip_norm):
        grad_in = jnp.einsum('ti,ktj->kij', x_norm, dy_in, preferred_element_type=jnp.float32)
        grad_out = jnp.einsum('ti,tj->ij', hid_act, dy_out, preferred_element_type=jnp.float32)
        totals_in = lax.psum(local_sums(grad_in, w_in, row_in), 'tp')
        totals_out = lax.psum(local_sums(grad_out, w_out, row_out), 'tp')
        norm_sq = jnp.sum(totals_in[..., :-2]) + jnp.sum(totals_out[..., :-2])
        grad_scale = jnp.minimum(1.0, clip_norm / jnp.sqrt(norm_sq))
        new_in = apply_update(w_in, grad_in, row_in, col_in, totals_in, shards, beta_two, rel_step, clip_rms, grad_scale)
        new_out = apply_update(w_out, grad_out, row_out, col_out, totals_out, shards, beta_two, rel_step, clip_rms, grad_scale)
        return new_in + new_out

    in_specs = (P(None, 'tp'), P(None, 'tp'), P(), P(), P(None, 'tp', None), P('tp', None),
                P(None, 'tp'), P(), P('tp'), P(), P(), P(), P(), P())
    out_specs = (P(None, 'tp', None), P(None, 'tp'), P(), P('tp', None), P('tp'), P())
    return jax.shard_map(local_step, mesh=mesh, in_specs=in_specs, out_specs=out_specs, check_vma=False)
```

profile of v0, /device:TPU:0, one launch (start us, length us, event | category | flops | bytes accessed | tf_op | source)
XLA Modules:
  0.0 144.2 jit_solution(2786034885441986389)
XLA Ops:
  0.7 1.6 %copy-done = bf16[8192,128]{1,0:T(8,128)(2,1)S(1)} copy-done((bf16[8192,128]{1,0:T(8,128)(2,1)S(1)}, bf16[8192,128]{1,0:T(8,128)(2,1)}, u32[]{:S(2)}) %copy-start) | copy-done | bytes 2097176
  2.2 36.8 %multiply_reduce_fusion.2 = (f32[2,2816]{1,0:T(2,128)S(1)}, f32[2,2816,128]{2,1,0:T(8,128)}) fusion(bf16[2,8192,2816]{2,1,0:T(8,128)(2,1)} %param.16, bf16[8192,128]{1,0:T(8,128)(2,1)S(1)} %copy-done), kind=kOutput, calls=%fused_computation.7 | convolution fusion | flops 11812595712 | bytes 97277952 | tf_op jit(solution)/shard_map/ti,ktj->kij/dot_general | solution.py:45
  39.1 0.1 reduce_sum.122
  39.2 0.1 copy.44
  39.3 2.3 %multiply_reduce_fusion.1 = f32[2]{0:T(128)S(1)} fusion(f32[2,128,2816]{2,1,0:T(8,128)} %param.18), kind=kLoop, calls=%fused_computation.6 | loop fusion | flops 1441790 | bytes 2883592 | tf_op jit(solution)/shard_map/reduce_sum | solution.py:13
  41.6 0.1 copy.45
  41.7 0.7 concatenate.6
  42.4 11.6 %multiply_reduce_fusion.5 = (f32[1024]{0:T(1024)S(1)}, f32[352,1024]{1,0:T(8,128)S(1)}) fusion(bf16[8192,352]{0,1:T(8,128)(2,1)} %param.15, bf16[8192,1024]{1,0:T(8,128)(2,1)} %param.17), kind=kOutput, calls=%fused_computation.15 | convolution fusion | flops 5906299904 | bytes 23990272 | tf_op jit(solution)/shard_map/ti,tj->ij/dot_general | solution.py:46
  54.0 0.6 reduce_sum.126
  54.6 2.3 %multiply_reduce_fusion.4 = f32[]{:T(128)} fusion(f32[352,1024]{1,0:T(8,128)} %param.19), kind=kLoop, calls=%fused_computation.14 | loop fusion | flops 720895 | bytes 1441796 | tf_op jit(solution)/shard_map/reduce_sum | solution.py:13
  56.9 1.4 concatenate.7
  58.3 26.0 %all-reduce.1 = (f32[2,2818]{1,0:T(2,128)}, f32[1026]{0:T(1024)S(1)}) all-reduce(f32[2,2818]{1,0:T(2,128)} %concatenate.6, f32[1026]{0:T(1024)S(1)} %concatenate.7), channel_id=1, replica_groups=mesh['tp'=8] {'tp'}, use_global_device_ids=true, to_apply=%region_3.0 | all-reduce | flops 6662 | bytes 53296 | tf_op jit(solution)/shard_map/psum | solution.py:47
  84.3 1.4 slice_reduce_fusion
  85.7 0.6 slice_reduce_fusion.2
  89.6 0.6 fusion.11
  90.9 0.3 add_reduce_fusion
  91.1 1.3 broadcast_divide_fusion
  92.4 0.7 multiply_add_fusion.1
  93.1 1.3 multiply_reduce_fusion.3
  94.4 0.7 multiply_bitcast_fusion
  95.1 0.1 copy.46
  95.8 1.5 %fusion.9 = (f32[2]{0:T(128)}, f32[2]{0:T(128)}) fusion(f32[2,2818]{1,0:T(2,128)} %get-tuple-element.36, f32[]{:T(128)} %copy.51, f32[2,1]{1,0:T(2,128)S(1)} %copy.46, f32[]{:T(128)} %copy.50), kind=kLoop, calls=%fused_computation.31 | loop fusion | flops 12 | bytes 48 | tf_op jit(solution)/shard_map/mul | solution.py:37
  97.3 2.2 %fusion.1 = f32[2,128]{1,0:T(2,128)S(1)} fusion(f32[2,2816,128]{2,1,0:T(8,128)} %get-tuple-element.45, f32[]{:T(128)S(6)} %min.3), kind=kLoop, calls=%fused_computation.3 | loop fusion | flops 2883328 | bytes 2884612 | tf_op jit(solution)/shard_map/reduce_sum | solution.py:27
  99.5 1.3 broadcast_divide_fusion.1
  100.8 0.8 multiply_add_fusion
  101.6 0.6 copy-done.1
  102.2 2.4 %multiply_reduce_fusion = f32[2]{0:T(128)S(1)} fusion(f32[2,2816,128]{2,1,0:T(8,128)} %get-tuple-element.45, f32[2,2816]{1,0:T(2,128)S(1)} %multiply_add_fusion, f32[2,128]{1,0:T(2,128)S(1)} %get-tuple-element.40, f32[]{:T(128)S(6)} %min.3), kind=kLoop, calls=%fused_computation.5 | loop fusion | flops 3604478 | bytes 2907148 | tf_op jit(solution)/shard_map/reduce_sum | solution.py:33
  104.6 23.6 %all-reduce = (f32[2]{0:T(128)}, f32[]{:T(128)}) all-reduce(f32[2]{0:T(128)S(1)} %multiply_reduce_fusion, f32[]{:T(128)} %multiply_reduce_fusion.3), channel_id=1, replica_groups=mesh['tp'=8] {'tp'}, use_global_device_ids=true, to_apply=%region_13.0 | all-reduce | flops 3 | bytes 24 | tf_op jit(solution)/shard_map/psum | solution.py:33
  130.3 2.9 %multiply_subtract_fusion.1 = f32[352,1024]{1,0:T(8,128)} fusion(f32[352,1024]{1,0:T(8,128)} %param.19, f32[352,1024]{1,0:T(8,128)S(1)} %get-tuple-element.47, f32[]{:T(128)S(6)} %max.27, f32[1024]{0:T(1024)S(1)} %multiply_add_fusion.1, f32[352]{0:T(512)S(1)} %get-tuple-element.38, f32[]{:T(128)S(6)} %min.3, f32[]{:T(128)} %bitcast.9), kind=kLoop, calls=%fused_computation.10 | loop fusion | flops 2162688 | bytes 4330892 | tf_op jit(solution)/shard_map/sub | solution.py:38
  133.2 3.4 %copy.47 = f32[2,128,2816]{1,2,0:T(8,128)} copy(f32[2,128,2816]{2,1,0:T(8,128)} %param.18) | data formatting | bytes 5767168 | tf_op args[4]
  136.6 4.3 %multiply_subtract_fusion = f32[2,128,2816]{1,2,0:T(8,128)} fusion(f32[2,128,2816]{1,2,0:T(8,128)} %copy.47, f32[2,2816,128]{2,1,0:T(8,128)} %get-tuple-element.45, f32[2]{0:T(128)S(1)} %divide_maximum_fusion, f32[2,2816]{1,0:T(2,128)S(1)} %copy-done.2, f32[2,128]{1,0:T(2,128)S(1)} %get-tuple-element.40, f32[]{:T(128)S(6)} %min.3, f32[2]{0:T(128)S(1)} %copy-done.6), kind=kLoop, calls=%fused_computation.4 | loop fusion | flops 4325376 | bytes 8674324 | tf_op jit(solution)/shard_map/sub | solution.py:38
  140.9 3.4 %copy.48 = f32[2,128,2816]{2,1,0:T(8,128)} copy(f32[2,128,2816]{1,2,0:T(8,128)} %multiply_subtract_fusion) | data formatting | bytes 5767168
  (15 shorter events, 0.0 us)
Async XLA Ops:
  0.6 1.6 %copy-start = (bf16[8192,128]{1,0:T(8,128)(2,1)S(1)}, bf16[8192,128]{1,0:T(8,128)(2,1)}, u32[]{:S(2)}) copy-start(bf16[8192,128]{1,0:T(8,128)(2,1)} %param.14) | copy-start | bytes 6291460
  0.6 38.4 %copy-start.5 = (f32[2,128]{1,0:T(2,128)S(1)}, f32[2,128]{1,0:T(2,128)}, u32[]{:S(2)}) copy-start(f32[2,128]{1,0:T(2,128)} %param.20) | copy-start | bytes 3076
  42.4 11.6 %copy-start.4 = (f32[352]{0:T(512)S(1)}, f32[352]{0:T(512)}, u32[]{:S(2)}) copy-start(f32[352]{0:T(512)} %param.22) | copy-start | bytes 4228
  93.1 37.2 %copy-start.3 = (f32[1024]{0:T(1024)}, f32[1024]{0:T(1024)S(1)}, u32[]{:S(2)}) copy-start(f32[1024]{0:T(1024)S(1)} %multiply_add_fusion.1) | copy-start | bytes 12292
  101.6 0.6 copy-start.1
  128.2 5.0 %copy-start.7 = (f32[2]{0:T(128)S(1)}, f32[2]{0:T(128)}, u32[]{:S(2)}) copy-start(f32[2]{0:T(128)} %get-tuple-element.34) | copy-start | bytes 28
  133.2 3.4 %copy-start.2 = (f32[2,2816]{1,0:T(2,128)S(1)}, f32[2,2816]{1,0:T(2,128)}, u32[]{:S(2)}) copy-start(f32[2,2816]{1,0:T(2,128)} %copy-done.1) | copy-start | bytes 67588
  133.2 3.4 %copy-start.6 = (f32[2]{0:T(128)S(1)}, f32[2]{0:T(128)}, u32[]{:S(2)}) copy-start(f32[2]{0:T(128)} %get-tuple-element.30) | copy-start | bytes 28
where the time goes:
time: 145 us; the launch traced here: 144 us
  blocking collectives  49.6 us (34%)
  matrix products  48.4 us (33%)
  other arithmetic  26.8 us (18%)
  local copies, waits for them, and re-layouts  12 us (8%)
  between operations  7.42 us (5%)
    dot_general x1, matrix products, local_step(): jnp.einsum('ti,ktj->kij', x_norm, dy_in, preferred_element_type=jnp.float32)  36.8 us
    psum x1, blocking collectives, local_step(): totals_in = lax.psum(local_sums(grad_in, w_in, row_in), 'tp')  26 us
    psum x1, blocking collectives, apply_update(): upd_sq = lax.psum(jnp.sum(update * update, axis=(-2, -1)), 'tp')  23.6 us
    dot_general x1, matrix products, local_step(): jnp.einsum('ti,tj->ij', hid_act, dy_out, preferred_element_type=jnp.float32)  11.6 us
    unnamed x18, local copies, waits for them, and re-layouts  8.96 us
    sub x2, other arithmetic, apply_update(): return (weight - step_size * clipped, row_new, col_new)  7.12 us
    reduce_sum x2, other arithmetic, local_sums(): w_sq = jnp.sum(weight * weight, axis=(-2, -1))[..., None]  4.62 us
    reduce_sum x2, other arithmetic, apply_update(): upd_sq = lax.psum(jnp.sum(update * update, axis=(-2, -1)), 'tp')  3.72 us

commit v1 on v0

v1 whole, which is shorter than its diff:
```python
import jax
import jax.numpy as jnp
from jax import lax
from jax.experimental import pallas as pl
from jax.experimental.pallas import tpu as pltpu
from jax.sharding import PartitionSpec as P

EPS_ONE = 1e-30
EPS_TWO = 1e-3
MESH = pl.DeviceIdType.MESH
F32 = jnp.float32

T = 8192
D = 1024
FF = 2816
ND = 8
XR = D // ND
HR = FF // ND
KC = 1024
NC = T // KC
NB_IN = FF // 128
NB_OUT = D // 128
ROWS_OUT = ((0, 128), (128, 128), (256, HR - 256))


def total(v):
    return jnp.sum(jnp.sum(v, axis=0, keepdims=True), axis=1, keepdims=True)


def spread(row):
    return jnp.broadcast_to(row, (128, row.shape[1])).T


def unspread(col):
    return jnp.broadcast_to(col, (128, 128)).T[0:1, :]


def grad_kernel(x_hbm, hid_hbm, dyi_hbm, dyo_hbm, wi_hbm, wo_hbm, ri_hbm, ci_hbm, ro_hbm, co_hbm,
                beta_hbm, rel_hbm, crms_hbm, cnorm_hbm,
                d_in, d_out, w_in, w_out, rin_new, cin_new, rout_new, cout_new, kappa,
                x_own, x_peer, xt, hid, ring, acc, grecv, m1, m2, m3, row_sq, rpad,
                ri, ci, ro, co, beta, rel, crms, cnorm,
                s_x, s_hid, s_dyo, s_dyi, s_w, s_small, xs_send, xs_recv, g_send, g_recv,
                m1_send, m1_recv, m2_send, m2_recv, m3_send, m3_recv):
    me = lax.axis_index("tp")
    core = lax.rem(me, 2)
    other = 1 - core
    peer = me + 1 - 2 * core

    def hid_copy(q):
        c = pl.ds(pl.multiple_of(q * KC, KC), KC)
        return pltpu.make_async_copy(hid_hbm.at[:, c], hid.at[:, c], s_hid.at[q])

    def dyo_copy(q, slot, half):
        return pltpu.make_async_copy(dyo_hbm.at[pl.ds(pl.multiple_of(q * KC, KC), KC), :],
                                     ring.at[slot, :, pl.ds(half * D, D)], s_dyo.at[q])

    def dyi_copy(i):
        return pltpu.make_async_copy(dyi_hbm.at[core, pl.ds(pl.multiple_of(i * KC, KC), KC), :],
                                     ring.at[lax.rem(i, 3)], s_dyi.at[lax.rem(i, 3)])

    def x_send(i):
        c = pl.ds(pl.multiple_of(i * KC, KC), KC)
        return pltpu.make_async_remote_copy(x_own.at[c, :], x_peer.at[c, :], xs_send.at[i], xs_recv.at[i],
                                            device_id=(peer,), device_id_type=MESH)

    def bcast(buf, send, recv):
        return [pltpu.make_async_remote_copy(buf.at[me], buf.at[me], send.at[k], recv.at[me],
                                             device_id=(lax.rem(me + k, ND),), device_id_type=MESH)
                for k in range(1, ND)]

    def arrivals(buf, send, recv):
        out = []
        for k in range(1, ND):
            src = lax.rem(me + k, ND)
            out.append(pltpu.make_async_remote_copy(buf.at[src], buf.at[src], send.at[k], recv.at[src],
                                                    device_id=(src,), device_id_type=MESH))
        return out

    def exchange_wait(buf, send, recv):
        for cp in arrivals(buf, send, recv):
            cp.wait_recv()

    x_load = pltpu.make_async_copy(x_hbm, x_own, s_x)
    x_load.start()
    hid_copy(0).start()
    dyo_copy(0, 2, 0).start()
    hid_copy(1).start()
    dyo_copy(1, 2, 1).start()
    dyi_copy(0).start()
    small = [pltpu.make_async_copy(a, b, s_small.at[n]) for n, (a, b) in enumerate(
        ((ri_hbm, ri), (ci_hbm, ci), (ro_hbm, ro), (co_hbm, co),
         (beta_hbm, beta), (rel_hbm, rel), (crms_hbm, crms), (cnorm_hbm, cnorm)))]
    for cp in small:
        cp.start()

    barrier = pltpu.get_barrier_semaphore()
    for k in range(1, ND):
        pl.semaphore_signal(barrier, inc=1, device_id=(lax.rem(me + k, ND),), device_id_type=MESH)
    acc[...] = jnp.zeros_like(acc)
    d_out[...] = jnp.zeros_like(d_out)
    m1[me, NB_IN:24, :] = jnp.zeros((24 - NB_IN, 128), F32)
    m2[me, 8:16, :] = jnp.zeros((8, 128), F32)
    rpad[...] = jnp.zeros_like(rpad)
    pl.semaphore_wait(barrier, ND - 1)

    x_load.wait()
    for i in range(NC):
        x_send(i).start()

    def out_step(q, slot, half):
        hid_copy(q).wait()
        dyo_copy(q, slot, half).wait()
        lhs = hid[:, pl.ds(q * KC, KC)]
        for n in range(D // 256):
            c = pl.ds(n * 256, 256)
            d_out[:, c] += jnp.dot(lhs, ring[slot, :, pl.ds(half * D + n * 256, 256)], preferred_element_type=F32)

    out_step(0, 2, 0)
    dyi_copy(1).start()
    out_step(1, 2, 1)
    dyi_copy(2).start()

    @pl.loop(0, NC)
    def _(i):
        slot = lax.rem(i, 3)
        rows = pl.ds(pl.multiple_of(i * KC, KC), KC)
        x_send(i).wait_recv()
        xt[0:XR, :] = x_own[rows, :].T
        xt[XR:2 * XR, :] = x_peer[rows, :].T
        dyi_copy(i).wait()
        for n in range(FF // 256):
            c = pl.ds(n * 256, 256)
            acc[:, c] += jnp.dot(xt[...], ring[slot, :, c], preferred_element_type=F32)

        @pl.when(i < NC - 3)
        def _():
            dyi_copy(i + 3).start()

        @pl.when(i >= NC - 3)
        def _():
            q = 2 * (i - (NC - 4))
            hid_copy(q).start()
            dyo_copy(q, slot, 0).start()
            hid_copy(q + 1).start()
            dyo_copy(q + 1, slot, 1).start()

    loads = [pltpu.make_async_copy(wi_hbm, w_in, s_w.at[0]), pltpu.make_async_copy(wo_hbm, w_out, s_w.at[1])]
    for cp in loads:
        cp.start()

    for j in range(NB_IN):
        g = acc[:, j * 128:(j + 1) * 128]
        m1[me, j:j + 1, :] = jnp.sum(g * g, axis=0, keepdims=True)
    g_copy = pltpu.make_async_remote_copy(acc.at[pl.ds(XR, XR), :], grecv, g_send, g_recv,
                                          device_id=(peer,), device_id_type=MESH)
    g_copy.start()
    m1_out = bcast(m1, m1_send, m1_recv)
    for cp in m1_out:
        cp.start()

    out_step(2, 2, 0)
    out_step(3, 2, 1)

    for cp in small:
        cp.wait()
    for cp in loads:
        cp.wait()
    for k in range(2):
        m2[me, 8 + k:9 + k, :] = ri[k:k + 1, :]
        w_sq = jnp.zeros((8, 128), F32)
        for j in range(NB_IN):
            w = w_in[k, :, j * 128:(j + 1) * 128]
            w_sq = w_sq + jnp.sum((w * w).reshape(XR // 8, 8, 128), axis=0)
        m2[me, 11 + k:12 + k, :] = jnp.sum(w_sq, axis=0, keepdims=True)
    rpad[:, 0:HR] = ro[...].reshape(1, HR)
    m2[me, 10:11, :] = rpad[:, 0:128] + rpad[:, 128:256] + rpad[:, 256:384]
    w_sq = jnp.zeros((8, 128), F32)
    for j in range(NB_OUT):
        w = w_out[:, j * 128:(j + 1) * 128]
        w_sq = w_sq + jnp.sum((w * w).reshape(HR // 8, 8, 128), axis=0)
    m2[me, 13:14, :] = jnp.sum(w_sq, axis=0, keepdims=True)

    out_step(4, 0, 0)
    out_step(5, 0, 1)

    g_copy.wait()
    for b, ref in enumerate((acc, grecv)):
        s = jnp.zeros((XR, 128), F32)
        for j in range(NB_IN):
            g = ref[0:XR, j * 128:(j + 1) * 128]
            s = s + g * g
        row_sq[b * 128:(b + 1) * 128, :] = jnp.broadcast_to(jnp.sum(s, axis=1, keepdims=True), (XR, 128))

    out_step(6, 1, 0)
    out_step(7, 1, 1)

    for j in range(NB_OUT):
        g = d_out[:, j * 128:(j + 1) * 128]
        m2[me, j:j + 1, :] = jnp.sum(g * g, axis=0, keepdims=True)
    m2_out = bcast(m2, m2_send, m2_recv)
    for cp in m2_out:
        cp.start()
    for lo, n in ROWS_OUT:
        s = jnp.zeros((n, 128), F32)
        for j in range(NB_OUT):
            g = d_out[lo:lo + n, j * 128:(j + 1) * 128]
            s = s + g * g
        row_sq[256 + lo:256 + lo + n, :] = jnp.broadcast_to(jnp.sum(s, axis=1, keepdims=True), (n, 128))

    exchange_wait(m1, m1_send, m1_recv)
    exchange_wait(m2, m2_send, m2_recv)

    b2 = beta[...]
    mix = 1.0 - b2
    col = [(m1[0] + m1[2]) + (m1[4] + m1[6]), (m1[1] + m1[3]) + (m1[5] + m1[7])]
    both = ((m2[0] + m2[1]) + (m2[2] + m2[3])) + ((m2[4] + m2[5]) + (m2[6] + m2[7]))
    col.append(both[0:8, :])
    scal = jnp.sum(both[8:16, :], axis=1, keepdims=True)
    tot = [total(v) for v in col]
    norm_sq = tot[0] + tot[1] + tot[2]
    gs = jnp.minimum(1.0, cnorm[...] / jnp.sqrt(norm_sq))

    shape = [(D, FF), (D, FF), (FF, D)]
    level = [b2 * scal[k:k + 1, :] / m + mix * (gs * (gs * tot[k]) / (m * n) + EPS_ONE)
             for k, (m, n) in enumerate(shape)]

    fac = []
    for k in range(3):
        nb = NB_IN if k < 2 else NB_OUT
        old = ([ci[k:k + 1, j * 128:(j + 1) * 128] for j in range(nb)] if k < 2
               else [co[:, j * 128:(j + 1) * 128] for j in range(nb)])
        rows = []
        for j in range(nb):
            new = b2 * old[j] + mix * (gs * (gs * col[k][j:j + 1, :]) / shape[k][0] + EPS_ONE)
            if k < 2:
                cin_new[k:k + 1, j * 128:(j + 1) * 128] = new
            else:
                cout_new[:, j * 128:(j + 1) * 128] = new
            rows.append(gs * lax.rsqrt(new))
        fac.append(rows)

    def row_factor(old, sq, lvl, n):
        new = b2 * old + mix * (gs * (gs * sq) / n + EPS_ONE)
        return new, lax.rsqrt(new / lvl)

    lane = lax.broadcasted_iota(jnp.int32, (1, 128), 1)
    m3[me] = jnp.zeros((8, 128), F32)

    def pick(a, b, first):
        return jnp.where(first, a, b)

    is0 = core == 0
    for b, ref in enumerate((acc, grecv)):
        first = is0 if b == 0 else jnp.logical_not(is0)
        t = [pick(fac[0][j], fac[1][j], first) for j in range(NB_IN)]
        old = pick(ri[0:1, :], ri[1:2, :], first)
        lvl = pick(level[0], level[1], first)
        new, fr = row_factor(spread(old), row_sq[b * 128:(b + 1) * 128, :], lvl, FF)
        s = jnp.zeros((XR, 128), F32)
        for j in range(NB_IN):
            v = ref[0:XR, j * 128:(j + 1) * 128] * t[j]
            s = s + v * v
        usq = jnp.sum(s * (fr * fr), axis=0, keepdims=True)
        k = core if b == 0 else other
        m3[me, pl.ds(k, 1), :] = usq
        row_sq[b * 128:(b + 1) * 128, :] = fr
        rin_new[pl.ds(k, 1), :] = new.T[0:1, :]
    usq = jnp.zeros((1, 128), F32)
    for lo, n in ROWS_OUT:
        old = spread(rpad[:, lo:lo + 128])[0:n, :]
        new, fr = row_factor(old, row_sq[256 + lo:256 + lo + n, :], level[2], D)
        s = jnp.zeros((n, 128), F32)
        for j in range(NB_OUT):
            v = d_out[lo:lo + n, j * 128:(j + 1) * 128] * fac[2][j]
            s = s + v * v
        usq = usq + jnp.sum(s * (fr * fr), axis=0, keepdims=True)
        row_sq[256 + lo:256 + lo + n, :] = fr
        if n < 128:
            new = jnp.concatenate([new, jnp.zeros((128 - n, 128), F32)], axis=0)
        rpad[:, lo:lo + 128] = new.T[0:1, :]
    m3[me, 2:3, :] = usq
    rout_new[...] = rpad[:, 0:HR].reshape(HR)

    m3_out = bcast(m3, m3_send, m3_recv)
    for cp in m3_out:
        cp.start()

    for b, ref in enumerate((acc, grecv)):
        first = is0 if b == 0 else jnp.logical_not(is0)
        k = core if b == 0 else other
        fr = row_sq[b * 128:(b + 1) * 128, :]
        for j in range(NB_IN):
            t = pick(fac[0][j], fac[1][j], first)
            d_in[k, :, j * 128:(j + 1) * 128] = ref[0:XR, j * 128:(j + 1) * 128] * t * fr
    for lo, n in ROWS_OUT:
        fr = row_sq[256 + lo:256 + lo + n, :]
        for j in range(NB_OUT):
            c = slice(j * 128, (j + 1) * 128)
            d_out[lo:lo + n, c] = d_out[lo:lo + n, c] * fac[2][j] * fr

    exchange_wait(m3, m3_send, m3_recv)
    usum = ((m3[0] + m3[1]) + (m3[2] + m3[3])) + ((m3[4] + m3[5]) + (m3[6] + m3[7]))
    urms = jnp.sqrt(jnp.sum(usum, axis=1, keepdims=True)[0:3, :] / (D * FF))
    wrms = jnp.sqrt(scal[3:6, :] / (D * FF))
    kap = rel[...] * jnp.maximum(EPS_TWO, wrms) / jnp.maximum(1.0, urms / crms[...])
    kappa[0:3, :] = jnp.broadcast_to(kap, (3, 128))
    kappa[3:8, :] = jnp.zeros((5, 128), F32)

    for i in range(NC):
        x_send(i).wait_send()
    for cp in m1_out + m2_out + m3_out:
        cp.wait_send()


def write_kernel(d_in, d_out, w_in, w_out, rin, cin, rout, cout, kappa,
                 wi_hbm, ri_hbm, ci_hbm, wo_hbm, ro_hbm, co_hbm, st_in, st_out, sem, sem_small):
    small = [pltpu.make_async_copy(a, b, sem_small.at[n]) for n, (a, b) in enumerate(
        ((rin, ri_hbm), (cin, ci_hbm), (rout, ro_hbm), (cout, co_hbm)))]
    for cp in small:
        cp.start()
    copies = []
    for k in range(2):
        kap = kappa[k:k + 1, :]
        for h in range(2):
            r = slice(h * 64, (h + 1) * 64)
            for j in range(NB_IN):
                c = slice(j * 128, (j + 1) * 128)
                st_in[k, r, c] = w_in[k, r, c] - kap * d_in[k, r, c]
            cp = pltpu.make_async_copy(st_in.at[k, pl.ds(h * 64, 64)], wi_hbm.at[k, pl.ds(h * 64, 64)],
                                       sem.at[2 * k + h])
            cp.start()
            copies.append(cp)
    kap = kappa[2:3, :]
    for h in range(2):
        r = slice(h * 176, (h + 1) * 176)
        for j in range(NB_OUT):
            c = slice(j * 128, (j + 1) * 128)
            st_out[r, c] = w_out[r, c] - kap * d_out[r, c]
        cp = pltpu.make_async_copy(st_out.at[pl.ds(h * 176, 176)], wo_hbm.at[pl.ds(h * 176, 176)], sem.at[4 + h])
        cp.start()
        copies.append(cp)
    for cp in copies + small:
        cp.wait()


def local_step(x_norm, hid_act, dy_in, dy_out, w_in, w_out, row_in, col_in, row_out, col_out,
               beta_two, rel_step, clip_rms, clip_norm):
    hbm = pl.BlockSpec(memory_space=pltpu.HBM)
    vmem = pl.BlockSpec(memory_space=pltpu.VMEM)
    dma = pltpu.SemaphoreType.DMA
    mids = [(2, XR, FF), (HR, D), (2, XR, FF), (HR, D), (2, XR), (2, FF), (HR,), (1, D), (8, 128)]
    mid = pl.pallas_call(
        grad_kernel,
        out_shape=[pltpu.VMEM(s, F32) for s in mids],
        in_specs=[hbm] * 14,
        out_specs=[vmem] * len(mids),
        scratch_shapes=[
            pltpu.VMEM((T, XR), jnp.bfloat16), pltpu.VMEM((T, XR), jnp.bfloat16),
            pltpu.VMEM((2 * XR, KC), jnp.bfloat16), pltpu.VMEM((HR, T), jnp.bfloat16),
            pltpu.VMEM((3, KC, FF), jnp.bfloat16), pltpu.VMEM((2 * XR, FF), F32), pltpu.VMEM((XR, FF), F32),
            pltpu.VMEM((ND, 24, 128), F32), pltpu.VMEM((ND, 16, 128), F32), pltpu.VMEM((ND, 8, 128), F32),
            pltpu.VMEM((256 + 384, 128), F32), pltpu.VMEM((1, 384), F32),
            pltpu.VMEM((2, XR), F32), pltpu.VMEM((2, FF), F32), pltpu.VMEM((HR,), F32), pltpu.VMEM((1, D), F32),
            pltpu.VMEM((1, 1), F32), pltpu.VMEM((1, 1), F32), pltpu.VMEM((1, 1), F32), pltpu.VMEM((1, 1), F32),
            dma(()), dma((NC,)), dma((NC,)), dma((3,)), dma((2,)), dma((8,)), dma((NC,)), dma((NC,)), dma(()), dma(()),
            dma((ND,)), dma((ND,)), dma((ND,)), dma((ND,)), dma((ND,)), dma((ND,)),
        ],
        compiler_params=pltpu.CompilerParams(collective_id=0, has_side_effects=True, vmem_limit_bytes=46 << 20),
        name="grad_stats",
    )(x_norm, hid_act.T, dy_in, dy_out, w_in, w_out, row_in, col_in,
      row_out, col_out.reshape(1, D),
      beta_two.reshape(1, 1), rel_step.reshape(1, 1), clip_rms.reshape(1, 1), clip_norm.reshape(1, 1))
    mid = [pltpu.with_memory_space_constraint(v, pltpu.VMEM) for v in mid]
    outs = [(2, XR, FF), (2, XR), (2, FF), (HR, D), (HR,), (1, D)]
    out = pl.pallas_call(
        write_kernel,
        out_shape=[pltpu.HBM(s, F32) for s in outs],
        in_specs=[vmem] * len(mids),
        out_specs=[hbm] * len(outs),
        scratch_shapes=[pltpu.VMEM((2, XR, FF), F32), pltpu.VMEM((HR, D), F32), dma((6,)), dma((4,))],
        compiler_params=pltpu.CompilerParams(vmem_limit_bytes=12 << 20),
        name="write_weights",
    )(*mid)
    return (out[0], out[1], out[2], out[3], out[4], out[5].reshape(D))


def solution(mesh):
    in_specs = (P(None, 'tp'), P(None, 'tp'), P(), P(), P(None, 'tp', None), P('tp', None),
                P(None, 'tp'), P(), P('tp'), P(), P(), P(), P(), P())
    out_specs = (P(None, 'tp', None), P(None, 'tp'), P(), P('tp', None), P('tp'), P())
    return jax.shard_map(local_step, mesh=mesh, in_specs=in_specs, out_specs=out_specs, check_vma=False)
```

time: 145 us -> 43 us (0.30)
  blocking collectives: 49.6 us -> 0 us
  matrix products: 48.4 us -> 0 us
  Pallas kernels: 0 us -> 39.7 us
  other arithmetic: 26.8 us -> 0 us
  local copies, waits for them, and re-layouts: 12 us -> 0 us
  between operations: 7.42 us -> 3.23 us
    psum x2 -> x0, blocking collectives: 49.6 us -> none  [the longest x1 26 us: local_step(): totals_in = lax.psum(local_sums(grad_in, w_in, row_in), 'tp')]
    dot_general x2 -> x0, matrix products: 48.4 us -> none  [the longest x1 36.8 us: local_step(): jnp.einsum('ti,ktj->kij', x_norm, dy_in, preferred_element_type=jnp.float32)]
    pallas_call x0 -> x2, Pallas kernels: none -> 39.7 us  [the longest x1 37.4 us: local_step(): pl.pallas_call(grad_kernel, out_shape=[pltpu.VMEM(s, F32) for s in mids],...]
    reduce_sum x10 -> x0, other arithmetic: 13.5 us -> none  [the longest x2 4.62 us: local_sums(): w_sq = jnp.sum(weight * weight, axis=(-2, -1))[..., None]]
    unnamed x18 -> x0, local copies, waits for them, and re-layouts: 8.96 us -> none
    sub x2 -> x0, other arithmetic: 7.12 us -> none  [apply_update(): return (weight - step_size * clipped, row_new, col_new)]
    div x2 -> x0, other arithmetic: 2.52 us -> none  [apply_update(): second = (row_new / row_level)[..., :, None] * col_new[..., None, :]]
    mul x2 -> x0, other arithmetic: 2.18 us -> none  [the longest x1 1.52 us: apply_update(): step_size = rel_step * jnp.maximum(EPS_TWO, w_rms)]
where the time goes in v1:
time: 43 us; the launch traced here: 42.9 us
  Pallas kernels  39.7 us (92%)
  between operations  3.23 us (8%)
    pallas_call x1, Pallas kernels, local_step(): pl.pallas_call(grad_kernel, out_shape=[pltpu.VMEM(s, F32) for s in mids],...  37.4 us
    pallas_call x1, Pallas kernels, local_step(): pl.pallas_call(write_kernel, out_shape=[pltpu.HBM(s, F32) for s in outs],...  2.22 us

profile of v1, /device:TPU:0, one launch (start us, length us, event | category | flops | bytes accessed | tf_op | source)
XLA Modules:
  0.0 42.9 jit_solution(17174325541719013450)
XLA Ops:
  3.2 37.4 %grad_stats.1 = (f32[2,128,2816]{2,1,0:T(8,128)S(1)}, f32[352,1024]{1,0:T(8,128)S(1)}, f32[2,128,2816]{2,1,0:T(8,128)S(1)}, f32[352,1024]{1,0:T(8,128)S(1)}, f32...) custom-call(bf16[8192,128]{1,0:T(8,128)(2,1)} %x_hbm.1, ...), custom_call_target="tpu_custom_call" | custom-call | tf_op jit(solution)/shard_map/grad_stats/pallas_call | solution.py:353
  40.7 2.2 %write_weights.1 = (f32[2,128,2816]{2,1,0:T(8,128)}, f32[2,128]{1,0:T(2,128)}, f32[2,2816]{1,0:T(2,128)}, f32[352,1024]{1,0:T(8,128)}, f32[352]{0:T(512)}, /*index=5*/f32[1,1024]{1,0:T(1,128)}) custom-call(f32[2,128,2816]{2,1,0:T(8,128)S(1)} %get-tuple-element.21.d_in, f32[352,1024]{1,0:T(8,128)S(1)} %get-tuple-element.22.d_out, ...), custom_call_target="tpu_custom_call" | custom-call | tf_op jit(solution)/shard_map/write_weights/pallas_call | solution.py:376

commit v2 on v0

v2 whole, which is shorter than its diff:
```python
import jax
import jax.numpy as jnp
from jax import lax
from jax.experimental import pallas as pl
from jax.experimental.pallas import tpu as pltpu
from jax.sharding import PartitionSpec as P

EPS_ONE = 1e-30
EPS_TWO = 1e-3
MESH = pl.DeviceIdType.MESH
F32 = jnp.float32

T = 8192
D = 1024
FF = 2816
ND = 8
XR = D // ND
HR = FF // ND
KC = 1024
NC = T // KC
L = 128
NB_IN = FF // L
NB_OUT = D // L
NP = 24
ROWS_OUT = ((0, L), (L, L), (2 * L, HR - 2 * L))
TILE = 2 * L
PIECES = ((0, 0, 0), (KC, 0, D), (2 * KC, 0, 0), (3 * KC, 0, D), (4 * KC, 1, 0), (5 * KC, 1, D), (6 * KC, 2, 0), (7 * KC, 2, D))
HEAD = 2


def total(v):
    return jnp.sum(jnp.sum(v, axis=0, keepdims=True), axis=1, keepdims=True)


def spread(row):
    return jnp.broadcast_to(row, (L, row.shape[1])).T


def grad_kernel(x_hbm, hid_hbm, dyi_hbm, dyo_hbm, wi_hbm, wo_hbm, ri_hbm, ci_hbm, ro_hbm, co_hbm,
                beta_hbm, rel_hbm, crms_hbm, cnorm_hbm,
                d_in, d_out, w_in, w_out, rin_new, cin_new, rout_new, cout_new, kappa,
                x_own, x_peer, xt0, xt1, hid, ring, acc, grecv, g2, m1, m2, m3, m4, row_sq, r_old, fac, c_old, rpad,
                ri, ci, ro, co, beta, rel, crms, cnorm,
                s_x, s_hid, s_dyo, s_dyi, s_w, s_small, xs_send, xs_recv, g_send, g_recv,
                m1_send, m1_recv, m2_send, m2_recv, m3_send, m3_recv, m4_send, m4_recv):
    me = lax.axis_index("tp")
    chip = me // 2
    core = me - 2 * chip
    other = 1 - core
    peer = 2 * chip + other
    diag = 3 - chip
    xn = chip + 1 - 2 * lax.rem(chip, 2)
    yn = lax.rem(chip + 2, 4)
    others = [2 * diag + core, 2 * diag + other, 2 * xn + core, 2 * yn + core, 2 * xn + other, 2 * yn + other, peer]

    def out_copies(p):
        k0, slot, c0 = PIECES[p]
        rows = pl.ds(k0, KC)
        return (pltpu.make_async_copy(hid_hbm.at[:, rows], hid.at[:, rows], s_hid.at[p]),
                pltpu.make_async_copy(dyo_hbm.at[rows, :], ring.at[slot, :, pl.ds(c0, D)], s_dyo.at[p]))

    def start_out(*ps):
        for p in ps:
            for cp in out_copies(p):
                cp.start()

    def dyi_copy(i):
        return pltpu.make_async_copy(dyi_hbm.at[core, pl.ds(i * KC, KC), :], ring.at[(i + 1) % 3], s_dyi.at[i])

    def x_send(i):
        c = pl.ds(i * KC, KC)
        return pltpu.make_async_remote_copy(x_own.at[c, :], x_peer.at[c, :], xs_send.at[i], xs_recv.at[i],
                                            device_id=(peer,), device_id_type=MESH)

    def bcast(buf, send, recv):
        out = [pltpu.make_async_remote_copy(buf.at[me], buf.at[me], send.at[k], recv.at[me],
                                            device_id=(dst,), device_id_type=MESH) for k, dst in enumerate(others)]
        for cp in out:
            cp.start()
        return out

    def exchange_wait(buf, send, recv):
        for k, src in reversed(list(enumerate(others))):
            pltpu.make_async_remote_copy(buf.at[src], buf.at[src], send.at[k], recv.at[src],
                                         device_id=(src,), device_id_type=MESH).wait_recv()

    start_out(0)
    x_load = pltpu.make_async_copy(x_hbm, x_own, s_x)
    x_load.start()
    start_out(1)
    dyi_copy(0).start()
    small = [pltpu.make_async_copy(a, b, s_small.at[n]) for n, (a, b) in enumerate(
        ((ri_hbm, ri), (ci_hbm, ci), (ro_hbm, ro), (co_hbm, co),
         (beta_hbm, beta), (rel_hbm, rel), (crms_hbm, crms), (cnorm_hbm, cnorm)))]
    for cp in small:
        cp.start()

    barrier = pltpu.get_barrier_semaphore()
    for dst in others:
        pl.semaphore_signal(barrier, inc=1, device_id=(dst,), device_id_type=MESH)
    rpad[...] = jnp.zeros_like(rpad)

    def wait_out(p):
        for cp in out_copies(p):
            cp.wait()

    def out_step(p, *extra):
        k0, slot, c0 = PIECES[p]
        lhs = hid[:, pl.ds(k0, KC)]
        for n in range(D // TILE):
            c = pl.ds(n * TILE, TILE)
            v = jnp.dot(lhs, ring[slot, :, pl.ds(c0 + n * TILE, TILE)], preferred_element_type=F32)
            d_out[:, c] = v if p == 0 else d_out[:, c] + v
            if n < len(extra):
                extra[n]()

    xt = (xt0, xt1)
    QT = KC // 4

    def transpose(i, n):
        rows = pl.ds(i * KC + n * QT, QT)
        cols = slice(n * QT, (n + 1) * QT)
        xt[i % 2][0:XR, cols] = x_own[rows, :].T
        xt[i % 2][XR:2 * XR, cols] = x_peer[rows, :].T

    own, both = slice(0, XR), slice(0, 2 * XR)
    blocks = [(both, n * TILE) for n in range(FF // TILE - 1)] + [(own, FF - TILE), (slice(XR, 2 * XR), FF - TILE)]

    def in_step(i):
        for n, (rows, c0) in enumerate(blocks):
            c = slice(c0, c0 + TILE)
            v = jnp.dot(xt[i % 2][rows, :], ring[(i + 1) % 3, :, c], preferred_element_type=F32)
            acc[rows, c] = v if i == 0 else acc[rows, c] + v
            if n < 4 and i + 1 < NC:
                transpose(i + 1, n)

    wait_out(0)
    out_step(0)
    dyi_copy(1).start()
    pl.semaphore_wait(barrier, ND - 1)
    x_load.wait()
    for i in range(NC):
        x_send(i).start()
    wait_out(1)
    out_step(1)
    dyi_copy(2).start()
    x_send(0).wait_recv()
    for n in range(4):
        transpose(0, n)
    for i in range(NC):
        if i + 1 < NC:
            x_send(i + 1).wait_recv()
        dyi_copy(i).wait()
        in_step(i)
        if i + 3 < NC:
            dyi_copy(i + 3).start()
        else:
            p = HEAD + 2 * (i + 3 - NC)
            start_out(p, p + 1)

    loads = [pltpu.make_async_copy(wi_hbm, w_in, s_w.at[0]), pltpu.make_async_copy(wo_hbm, w_out, s_w.at[1])]
    for cp in loads:
        cp.start()

    def stats_early():
        for j in range(NB_IN):
            g = acc[:, j * L:(j + 1) * L]
            m1[me, j:j + 1, :] = jnp.sum(g * g, axis=0, keepdims=True)
        rpad[:, 0:HR] = ro[...].reshape(1, HR)
        m1[me, NB_IN:NP, :] = jnp.zeros((NP - NB_IN, L), F32)
        m1[me, NP:26, :] = ri[...]
        m1[me, 26:27, :] = rpad[:, 0:L] + rpad[:, L:2 * L] + rpad[:, 2 * L:3 * L]
        m1[me, 27:32, :] = jnp.zeros((5, L), F32)

    for cp in small:
        cp.wait()
    wait_out(2)
    out_step(2, stats_early)
    g_copy = pltpu.make_async_remote_copy(acc.at[pl.ds(XR, XR), :], grecv, g_send, g_recv,
                                          device_id=(peer,), device_id_type=MESH)
    g_copy.start()
    m1_out = bcast(m1, m1_send, m1_recv)

    def stats_own(b, ref):
        def body():
            s = jnp.zeros((XR, L), F32)
            for j in range(NB_IN):
                c = slice(j * L, (j + 1) * L)
                g = ref[0:XR, c]
                g = g * g
                g2[b * L:(b + 1) * L, c] = g
                s = s + g
            row_sq[b * L:(b + 1) * L, :] = jnp.broadcast_to(jnp.sum(s, axis=1, keepdims=True), (XR, L))
        return body

    def old_stats():
        for k in range(2):
            r_old[k * L:(k + 1) * L, :] = spread(ri[k:k + 1, :])
            for j in range(NB_IN):
                c_old[k, j:j + 1, :] = ci[k:k + 1, j * L:(j + 1) * L]
            c_old[k, NB_IN:NP, :] = jnp.ones((NP - NB_IN, L), F32)
        for lo in (0, L, 2 * L):
            r_old[2 * L + lo:3 * L + lo, :] = spread(rpad[:, lo:lo + L])
        for j in range(NB_OUT):
            c_old[2, j:j + 1, :] = co[:, j * L:(j + 1) * L]

    wait_out(3)
    out_step(3, stats_own(0, acc))
    wait_out(4)
    out_step(4, old_stats)
    wait_out(5)
    g_copy.wait()
    out_step(5, stats_own(1, grecv))
    wait_out(6)
    out_step(6)
    wait_out(7)
    out_step(7)

    for j in range(NB_OUT):
        g = d_out[:, j * L:(j + 1) * L]
        m2[me, j:j + 1, :] = jnp.sum(g * g, axis=0, keepdims=True)
    m2_out = bcast(m2, m2_send, m2_recv)

    for lo, n in ROWS_OUT:
        s = jnp.zeros((n, L), F32)
        for j in range(NB_OUT):
            c = slice(j * L, (j + 1) * L)
            g = d_out[lo:lo + n, c]
            g = g * g
            g2[2 * L + lo:2 * L + lo + n, c] = g
            s = s + g
        row_sq[2 * L + lo:2 * L + lo + n, :] = jnp.broadcast_to(jnp.sum(s, axis=1, keepdims=True), (n, L))
    for cp in loads:
        cp.wait()
    m4[me] = jnp.zeros((8, L), F32)
    for k in range(2):
        w_sq = jnp.zeros((8, L), F32)
        for j in range(NB_IN):
            w = w_in[k, :, j * L:(j + 1) * L]
            w_sq = w_sq + jnp.sum((w * w).reshape(XR // 8, 8, L), axis=0)
        m4[me, k:k + 1, :] = jnp.sum(w_sq, axis=0, keepdims=True)
    w_sq = jnp.zeros((8, L), F32)
    for j in range(NB_OUT):
        w = w_out[:, j * L:(j + 1) * L]
        w_sq = w_sq + jnp.sum((w * w).reshape(HR // 8, 8, L), axis=0)
    m4[me, 2:3, :] = jnp.sum(w_sq, axis=0, keepdims=True)

    exchange_wait(m1, m1_send, m1_recv)
    b2 = beta[...]
    mix = 1.0 - b2
    col = [(m1[0, 0:NP] + m1[2, 0:NP]) + (m1[4, 0:NP] + m1[6, 0:NP]),
           (m1[1, 0:NP] + m1[3, 0:NP]) + (m1[5, 0:NP] + m1[7, 0:NP])]
    tail = slice(NP, 32)
    scal = ((m1[0, tail] + m1[1, tail]) + (m1[2, tail] + m1[3, tail])) + (
        (m1[4, tail] + m1[5, tail]) + (m1[6, tail] + m1[7, tail]))
    scal = jnp.sum(scal, axis=1, keepdims=True)
    tot = [total(v) for v in col]
    exchange_wait(m2, m2_send, m2_recv)
    col.append(((m2[0] + m2[1]) + (m2[2] + m2[3])) + ((m2[4] + m2[5]) + (m2[6] + m2[7])))
    tot.append(total(col[2]))
    norm_sq = tot[0] + tot[1] + tot[2]
    gs = jnp.minimum(1.0, cnorm[...] / jnp.sqrt(norm_sq))

    shape = [(D, FF), (D, FF), (FF, D)]
    level = [b2 * scal[k:k + 1, :] / m + mix * (gs * (gs * tot[k]) / (m * n) + EPS_ONE)
             for k, (m, n) in enumerate(shape)]

    for k in range(3):
        nb = NP if k < 2 else NB_OUT
        new = b2 * c_old[k, 0:nb] + mix * (gs * (gs * col[k]) / shape[k][0] + EPS_ONE)
        c_old[k, 0:nb] = new
        t = gs * lax.rsqrt(new)
        fac[k, 0:nb] = t
        fac[3 + k, 0:nb] = t * t

    def row_factor(old, rows, lvl, n):
        new = b2 * old + mix * (gs * (gs * row_sq[rows, :]) / n + EPS_ONE)
        return new, lax.rsqrt(new / lvl)

    is0 = core == 0
    ks = (core, other)
    for b in range(2):
        rows = slice(b * L, (b + 1) * L)
        lvl = jnp.where(is0 if b == 0 else jnp.logical_not(is0), level[0], level[1])
        new, fr = row_factor(r_old[pl.ds(pl.multiple_of(ks[b] * L, L), L), :], rows, lvl, FF)
        s = jnp.zeros((XR, L), F32)
        for j in range(NB_IN):
            s = s + g2[rows, j * L:(j + 1) * L] * fac[3 + ks[b], j:j + 1, :]
        m3[me, pl.ds(ks[b], 1), :] = jnp.sum(s * (fr * fr), axis=0, keepdims=True)
        row_sq[rows, :] = fr
        r_old[pl.ds(pl.multiple_of(ks[b] * L, L), L), :] = new
    usq = jnp.zeros((1, L), F32)
    for lo, n in ROWS_OUT:
        rows = slice(2 * L + lo, 2 * L + lo + n)
        new, fr = row_factor(r_old[rows, :], rows, level[2], D)
        s = jnp.zeros((n, L), F32)
        for j in range(NB_OUT):
            s = s + g2[rows, j * L:(j + 1) * L] * fac[5, j:j + 1, :]
        usq = usq + jnp.sum(s * (fr * fr), axis=0, keepdims=True)
        row_sq[rows, :] = fr
        r_old[rows, :] = new
    m3[me, 2:3, :] = usq
    m3[me, 3:4, :] = jnp.zeros((1, L), F32)
    m3_out = bcast(m3, m3_send, m3_recv)
    m4_out = bcast(m4, m4_send, m4_recv)

    for b, ref in enumerate((acc, grecv)):
        fr = row_sq[b * L:(b + 1) * L, :]
        for j in range(NB_IN):
            c = slice(j * L, (j + 1) * L)
            d_in[ks[b], :, c] = ref[0:XR, c] * fac[ks[b], j:j + 1, :] * fr
    for lo, n in ROWS_OUT:
        fr = row_sq[2 * L + lo:2 * L + lo + n, :]
        for j in range(NB_OUT):
            c = slice(j * L, (j + 1) * L)
            d_out[lo:lo + n, c] = d_out[lo:lo + n, c] * fac[2, j:j + 1, :] * fr
    for k in range(2):
        rin_new[k:k + 1, :] = r_old[k * L:(k + 1) * L, :].T[0:1, :]
        for j in range(NB_IN):
            cin_new[k:k + 1, j * L:(j + 1) * L] = c_old[k, j:j + 1, :]
    for lo in (0, L, 2 * L):
        rpad[:, lo:lo + L] = r_old[2 * L + lo:3 * L + lo, :].T[0:1, :]
    rout_new[...] = rpad[:, 0:HR].reshape(HR)
    for j in range(NB_OUT):
        cout_new[:, j * L:(j + 1) * L] = c_old[2, j:j + 1, :]

    exchange_wait(m4, m4_send, m4_recv)
    wsum = ((m4[0] + m4[1]) + (m4[2] + m4[3])) + ((m4[4] + m4[5]) + (m4[6] + m4[7]))
    wrms = jnp.sqrt(jnp.sum(wsum, axis=1, keepdims=True)[0:4, :] / (D * FF))
    step = rel[...] * jnp.maximum(EPS_TWO, wrms)
    exchange_wait(m3, m3_send, m3_recv)
    usum = ((m3[0] + m3[1]) + (m3[2] + m3[3])) + ((m3[4] + m3[5]) + (m3[6] + m3[7]))
    urms = jnp.sqrt(jnp.sum(usum, axis=1, keepdims=True) / (D * FF))
    kappa[0:4, :] = jnp.broadcast_to(step / jnp.maximum(1.0, urms / crms[...]), (4, L))
    kappa[4:8, :] = jnp.zeros((4, L), F32)

    for i in range(NC):
        x_send(i).wait_send()
    for cp in m1_out + m2_out + m3_out + m4_out:
        cp.wait_send()


def write_kernel(d_in, d_out, w_in, w_out, rin, cin, rout, cout, kappa,
                 wi_hbm, ri_hbm, ci_hbm, wo_hbm, ro_hbm, co_hbm, st_in, st_out, sem, sem_small):
    copies = []
    for k in range(2):
        kap = kappa[k:k + 1, :]
        for h in range(4):
            r = slice(h * 32, (h + 1) * 32)
            for j in range(NB_IN):
                c = slice(j * L, (j + 1) * L)
                st_in[k, r, c] = w_in[k, r, c] - kap * d_in[k, r, c]
            cp = pltpu.make_async_copy(st_in.at[k, pl.ds(h * 32, 32)], wi_hbm.at[k, pl.ds(h * 32, 32)],
                                       sem.at[4 * k + h])
            cp.start()
            copies.append(cp)
    small = [pltpu.make_async_copy(a, b, sem_small.at[n]) for n, (a, b) in enumerate(
        ((rin, ri_hbm), (cin, ci_hbm), (rout, ro_hbm), (cout, co_hbm)))]
    for cp in small:
        cp.start()
    kap = kappa[2:3, :]
    for h in range(4):
        r = slice(h * 88, (h + 1) * 88)
        for j in range(NB_OUT):
            c = slice(j * L, (j + 1) * L)
            st_out[r, c] = w_out[r, c] - kap * d_out[r, c]
        cp = pltpu.make_async_copy(st_out.at[pl.ds(h * 88, 88)], wo_hbm.at[pl.ds(h * 88, 88)], sem.at[8 + h])
        cp.start()
        copies.append(cp)
    for cp in copies + small:
        cp.wait()


def local_step(x_norm, hid_act, dy_in, dy_out, w_in, w_out, row_in, col_in, row_out, col_out,
               beta_two, rel_step, clip_rms, clip_norm):
    hbm = pl.BlockSpec(memory_space=pltpu.HBM)
    vmem = pl.BlockSpec(memory_space=pltpu.VMEM)
    dma = pltpu.SemaphoreType.DMA
    mids = [(2, XR, FF), (HR, D), (2, XR, FF), (HR, D), (2, XR), (2, FF), (HR,), (1, D), (8, L)]
    mid = pl.pallas_call(
        grad_kernel,
        out_shape=[pltpu.VMEM(s, F32) for s in mids],
        in_specs=[hbm] * 14,
        out_specs=[vmem] * len(mids),
        scratch_shapes=[
            pltpu.VMEM((T, XR), jnp.bfloat16), pltpu.VMEM((T, XR), jnp.bfloat16),
            pltpu.VMEM((2 * XR, KC), jnp.bfloat16), pltpu.VMEM((2 * XR, KC), jnp.bfloat16),
            pltpu.VMEM((HR, T), jnp.bfloat16), pltpu.VMEM((3, KC, FF), jnp.bfloat16),
            pltpu.VMEM((2 * XR, FF), F32), pltpu.VMEM((XR, FF), F32), pltpu.VMEM((2 * L + 3 * L, FF), F32),
            pltpu.VMEM((ND, 32, L), F32), pltpu.VMEM((ND, 8, L), F32), pltpu.VMEM((ND, 4, L), F32),
            pltpu.VMEM((ND, 8, L), F32), pltpu.VMEM((5 * L, L), F32), pltpu.VMEM((5 * L, L), F32),
            pltpu.VMEM((6, NP, L), F32), pltpu.VMEM((3, NP, L), F32), pltpu.VMEM((1, 3 * L), F32),
            pltpu.VMEM((2, XR), F32), pltpu.VMEM((2, FF), F32), pltpu.VMEM((HR,), F32), pltpu.VMEM((1, D), F32),
            pltpu.VMEM((1, 1), F32), pltpu.VMEM((1, 1), F32), pltpu.VMEM((1, 1), F32), pltpu.VMEM((1, 1), F32),
            dma(()), dma((len(PIECES),)), dma((len(PIECES),)), dma((NC,)), dma((2,)), dma((8,)), dma((NC,)), dma((NC,)),
            dma(()), dma(()), dma((ND,)), dma((ND,)), dma((ND,)), dma((ND,)), dma((ND,)), dma((ND,)), dma((ND,)),
            dma((ND,)),
        ],
        compiler_params=pltpu.CompilerParams(collective_id=0, has_side_effects=True, vmem_limit_bytes=50 << 20),
        name="grad_stats",
    )(x_norm, hid_act.T, dy_in, dy_out, w_in, w_out, row_in, col_in,
      row_out, col_out.reshape(1, D),
      beta_two.reshape(1, 1), rel_step.reshape(1, 1), clip_rms.reshape(1, 1), clip_norm.reshape(1, 1))
    mid = [pltpu.with_memory_space_constraint(v, pltpu.VMEM) for v in mid]
    outs = [(2, XR, FF), (2, XR), (2, FF), (HR, D), (HR,), (1, D)]
    out = pl.pallas_call(
        write_kernel,
        out_shape=[pltpu.HBM(s, F32) for s in outs],
        in_specs=[vmem] * len(mids),
        out_specs=[hbm] * len(outs),
        scratch_shapes=[pltpu.VMEM((2, XR, FF), F32), pltpu.VMEM((HR, D), F32), dma((12,)), dma((4,))],
        compiler_params=pltpu.CompilerParams(vmem_limit_bytes=12 << 20),
        name="write_weights",
    )(*mid)
    return (out[0], out[1], out[2], out[3], out[4], out[5].reshape(D))


def solution(mesh):
    in_specs = (P(None, 'tp'), P(None, 'tp'), P(), P(), P(None, 'tp', None), P('tp', None),
                P(None, 'tp'), P(), P('tp'), P(), P(), P(), P(), P())
    out_specs = (P(None, 'tp', None), P(None, 'tp'), P(), P('tp', None), P('tp'), P())
    return jax.shard_map(local_step, mesh=mesh, in_specs=in_specs, out_specs=out_specs, check_vma=False)
```

time: 145 us -> 40.6 us (0.28)
  blocking collectives: 49.6 us -> 0 us
  matrix products: 48.4 us -> 0 us
  Pallas kernels: 0 us -> 37.1 us
  other arithmetic: 26.8 us -> 0 us
  local copies, waits for them, and re-layouts: 12 us -> 0 us
  between operations: 7.42 us -> 3.39 us
    psum x2 -> x0, blocking collectives: 49.6 us -> none  [the longest x1 26 us: local_step(): totals_in = lax.psum(local_sums(grad_in, w_in, row_in), 'tp')]
    dot_general x2 -> x0, matrix products: 48.4 us -> none  [the longest x1 36.8 us: local_step(): jnp.einsum('ti,ktj->kij', x_norm, dy_in, preferred_element_type=jnp.float32)]
    pallas_call x0 -> x2, Pallas kernels: none -> 37.1 us  [the longest x1 34.8 us: local_step(): pl.pallas_call(grad_kernel, out_shape=[pltpu.VMEM(s, F32) for s in mids],...]
    reduce_sum x10 -> x0, other arithmetic: 13.5 us -> none  [the longest x2 4.62 us: local_sums(): w_sq = jnp.sum(weight * weight, axis=(-2, -1))[..., None]]
    unnamed x18 -> x0, local copies, waits for them, and re-layouts: 8.96 us -> none
    sub x2 -> x0, other arithmetic: 7.12 us -> none  [apply_update(): return (weight - step_size * clipped, row_new, col_new)]
    div x2 -> x0, other arithmetic: 2.52 us -> none  [apply_update(): second = (row_new / row_level)[..., :, None] * col_new[..., None, :]]
    mul x2 -> x0, other arithmetic: 2.18 us -> none  [the longest x1 1.52 us: apply_update(): step_size = rel_step * jnp.maximum(EPS_TWO, w_rms)]
where the time goes in v2:
time: 40.6 us; the launch traced here: 40.5 us
  Pallas kernels  37.1 us (91%)
  between operations  3.39 us (8%)
    pallas_call x1, Pallas kernels, local_step(): pl.pallas_call(grad_kernel, out_shape=[pltpu.VMEM(s, F32) for s in mids],...  34.8 us
    pallas_call x1, Pallas kernels, local_step(): pl.pallas_call(write_kernel, out_shape=[pltpu.HBM(s, F32) for s in outs],...  2.25 us

profile of v2, /device:TPU:0, one launch (start us, length us, event | category | flops | bytes accessed | tf_op | source)
XLA Modules:
  0.0 40.5 jit_solution(17292884247321384151)
XLA Ops:
  3.2 34.8 %grad_stats.1 = (f32[2,128,2816]{2,1,0:T(8,128)S(1)}, f32[352,1024]{1,0:T(8,128)S(1)}, f32[2,128,2816]{2,1,0:T(8,128)S(1)}, f32[352,1024]{1,0:T(8,128)S(1)}, f32...) custom-call(bf16[8192,128]{1,0:T(8,128)(2,1)} %x_hbm.1, ...), custom_call_target="tpu_custom_call" | custom-call | tf_op jit(solution)/shard_map/grad_stats/pallas_call | solution.py:380
  38.1 2.2 %write_weights.1 = (f32[2,128,2816]{2,1,0:T(8,128)}, f32[2,128]{1,0:T(2,128)}, f32[2,2816]{1,0:T(2,128)}, f32[352,1024]{1,0:T(8,128)}, f32[352]{0:T(512)}, /*index=5*/f32[1,1024]{1,0:T(1,128)}) custom-call(f32[2,128,2816]{2,1,0:T(8,128)S(1)} %get-tuple-element.21.d_in, f32[352,1024]{1,0:T(8,128)S(1)} %get-tuple-element.22.d_out, ...), custom_call_target="tpu_custom_call" | custom-call | tf_op jit(solution)/shard_map/write_weights/pallas_call | solution.py:406

commit v3 on v2

--- a/solution.py
+++ b/solution.py
@@ -24,8 +24,10 @@
 NP = 24
 ROWS_OUT = ((0, L), (L, L), (2 * L, HR - 2 * L))
 TILE = 2 * L
-PIECES = ((0, 0, 0), (KC, 0, D), (2 * KC, 0, 0), (3 * KC, 0, D), (4 * KC, 1, 0), (5 * KC, 1, D), (6 * KC, 2, 0), (7 * KC, 2, D))
+SLOTS = 4
+PARTS_OUT = ((0, 32), (32, 64), (96, L), (224, L))
 HEAD = 2
+PIECES = NC - HEAD
 
 
 def total(v):
@@ -39,9 +41,9 @@
 def grad_kernel(x_hbm, hid_hbm, dyi_hbm, dyo_hbm, wi_hbm, wo_hbm, ri_hbm, ci_hbm, ro_hbm, co_hbm,
                 beta_hbm, rel_hbm, crms_hbm, cnorm_hbm,
                 d_in, d_out, w_in, w_out, rin_new, cin_new, rout_new, cout_new, kappa,
-                x_own, x_peer, xt0, xt1, hid, ring, acc, grecv, g2, m1, m2, m3, m4, row_sq, r_old, fac, c_old, rpad,
+                x_own, x_peer, xt0, xt1, hid, ring, acc, grecv, g2, g2_out, go_send, go_recv, m1, m2, m3, m4, row_sq, r_old, fac, c_old, rpad,
                 ri, ci, ro, co, beta, rel, crms, cnorm,
-                s_x, s_hid, s_dyo, s_dyi, s_w, s_small, xs_send, xs_recv, g_send, g_recv,
+                s_x, s_hid, s_dyo, s_dyi, s_w, s_small, xs_send, xs_recv, hs_send, hs_recv, go_sems, g_send, g_recv,
                 m1_send, m1_recv, m2_send, m2_recv, m3_send, m3_recv, m4_send, m4_recv):
     me = lax.axis_index("tp")
     chip = me // 2
@@ -53,11 +55,21 @@
     yn = lax.rem(chip + 2, 4)
     others = [2 * diag + core, 2 * diag + other, 2 * xn + core, 2 * yn + core, 2 * xn + other, 2 * yn + other, peer]
 
+    def token(p, who):
+        return pl.multiple_of((who * HEAD + p) * KC, KC) if p < HEAD else (p + HEAD) * KC
+
+    def kept(p):
+        return p * KC if p < HEAD else (p + HEAD) * KC
+
     def out_copies(p):
-        k0, slot, c0 = PIECES[p]
-        rows = pl.ds(k0, KC)
-        return (pltpu.make_async_copy(hid_hbm.at[:, rows], hid.at[:, rows], s_hid.at[p]),
-                pltpu.make_async_copy(dyo_hbm.at[rows, :], ring.at[slot, :, pl.ds(c0, D)], s_dyo.at[p]))
+        rows = pl.ds(token(p, core), KC)
+        return (pltpu.make_async_copy(hid_hbm.at[:, rows], hid.at[:, pl.ds(kept(p), KC)], s_hid.at[p]),
+                pltpu.make_async_copy(dyo_hbm.at[rows, :], ring.at[p // 2, :, pl.ds(p % 2 * D, D)], s_dyo.at[p]))
+
+    def hid_send(p):
+        return pltpu.make_async_remote_copy(hid_hbm.at[:, pl.ds(token(p, other), KC)],
+                                            hid.at[:, pl.ds((HEAD + p) * KC, KC)], hs_send.at[p], hs_recv.at[p],
+                                            device_id=(peer,), device_id_type=MESH)
 
     def start_out(*ps):
         for p in ps:
@@ -65,7 +77,7 @@
                 cp.start()
 
     def dyi_copy(i):
-        return pltpu.make_async_copy(dyi_hbm.at[core, pl.ds(i * KC, KC), :], ring.at[(i + 1) % 3], s_dyi.at[i])
+        return pltpu.make_async_copy(dyi_hbm.at[core, pl.ds(i * KC, KC), :], ring.at[(i + 1) % SLOTS], s_dyi.at[i])
 
     def x_send(i):
         c = pl.ds(i * KC, KC)
@@ -89,6 +101,7 @@
     x_load.start()
     start_out(1)
     dyi_copy(0).start()
+    dyi_copy(1).start()
     small = [pltpu.make_async_copy(a, b, s_small.at[n]) for n, (a, b) in enumerate(
         ((ri_hbm, ri), (ci_hbm, ci), (ro_hbm, ro), (co_hbm, co),
          (beta_hbm, beta), (rel_hbm, rel), (crms_hbm, crms), (cnorm_hbm, cnorm)))]
@@ -105,14 +118,22 @@
             cp.wait()
 
     def out_step(p, *extra):
-        k0, slot, c0 = PIECES[p]
-        lhs = hid[:, pl.ds(k0, KC)]
         for n in range(D // TILE):
             c = pl.ds(n * TILE, TILE)
-            v = jnp.dot(lhs, ring[slot, :, pl.ds(c0 + n * TILE, TILE)], preferred_element_type=F32)
+            v = jnp.dot(hid[:, pl.ds(kept(p), KC)], ring[p // 2, :, pl.ds(p % 2 * D + n * TILE, TILE)],
+                        preferred_element_type=F32)
+            if p == HEAD:
+                v = v + go_recv[:, c]
             d_out[:, c] = v if p == 0 else d_out[:, c] + v
             if n < len(extra):
                 extra[n]()
+
+    def partner_step(p):
+        for n in range(D // TILE):
+            c = pl.ds(n * TILE, TILE)
+            v = jnp.dot(hid[:, pl.ds((HEAD + p) * KC, KC)], ring[0, :, pl.ds(p * D + n * TILE, TILE)],
+                        preferred_element_type=F32)
+            go_send[:, c] = v if p == 0 else go_send[:, c] + v
 
     xt = (xt0, xt1)
     QT = KC // 4
@@ -129,21 +150,28 @@
     def in_step(i):
         for n, (rows, c0) in enumerate(blocks):
             c = slice(c0, c0 + TILE)
-            v = jnp.dot(xt[i % 2][rows, :], ring[(i + 1) % 3, :, c], preferred_element_type=F32)
+            v = jnp.dot(xt[i % 2][rows, :], ring[(i + 1) % SLOTS, :, c], preferred_element_type=F32)
             acc[rows, c] = v if i == 0 else acc[rows, c] + v
             if n < 4 and i + 1 < NC:
                 transpose(i + 1, n)
 
+    go_copy = pltpu.make_async_remote_copy(go_send, go_recv, go_sems.at[0], go_sems.at[1],
+                                           device_id=(peer,), device_id_type=MESH)
+    pl.semaphore_wait(barrier, ND - 1)
+    for p in range(HEAD):
+        hid_send(p).start()
     wait_out(0)
     out_step(0)
-    dyi_copy(1).start()
-    pl.semaphore_wait(barrier, ND - 1)
     x_load.wait()
     for i in range(NC):
         x_send(i).start()
+    dyi_copy(2).start()
     wait_out(1)
     out_step(1)
-    dyi_copy(2).start()
+    for p in range(HEAD):
+        hid_send(p).wait_recv()
+        partner_step(p)
+    dyi_copy(3).start()
     x_send(0).wait_recv()
     for n in range(4):
         transpose(0, n)
@@ -152,11 +180,13 @@
             x_send(i + 1).wait_recv()
         dyi_copy(i).wait()
         in_step(i)
-        if i + 3 < NC:
+        if i == 0:
+            go_copy.start()
+        if i in (1, 3):
             dyi_copy(i + 3).start()
-        else:
-            p = HEAD + 2 * (i + 3 - NC)
-            start_out(p, p + 1)
+            dyi_copy(i + 4).start()
+        if i == NC - 3:
+            start_out(2, 3, 4, 5)
 
     loads = [pltpu.make_async_copy(wi_hbm, w_in, s_w.at[0]), pltpu.make_async_copy(wo_hbm, w_out, s_w.at[1])]
     for cp in loads:
@@ -175,10 +205,11 @@
     for cp in small:
         cp.wait()
     wait_out(2)
-    out_step(2, stats_early)
+    go_copy.wait()
     g_copy = pltpu.make_async_remote_copy(acc.at[pl.ds(XR, XR), :], grecv, g_send, g_recv,
                                           device_id=(peer,), device_id_type=MESH)
     g_copy.start()
+    out_step(2, stats_early)
     m1_out = bcast(m1, m1_send, m1_recv)
 
     def stats_own(b, ref):
@@ -209,12 +240,7 @@
     wait_out(4)
     out_step(4, old_stats)
     wait_out(5)
-    g_copy.wait()
-    out_step(5, stats_own(1, grecv))
-    wait_out(6)
-    out_step(6)
-    wait_out(7)
-    out_step(7)
+    out_step(5)
 
     for j in range(NB_OUT):
         g = d_out[:, j * L:(j + 1) * L]
@@ -227,9 +253,11 @@
             c = slice(j * L, (j + 1) * L)
             g = d_out[lo:lo + n, c]
             g = g * g
-            g2[2 * L + lo:2 * L + lo + n, c] = g
+            g2_out[lo:lo + n, c] = g
             s = s + g
         row_sq[2 * L + lo:2 * L + lo + n, :] = jnp.broadcast_to(jnp.sum(s, axis=1, keepdims=True), (n, L))
+    g_copy.wait()
+    stats_own(1, grecv)()
     for cp in loads:
         cp.wait()
     m4[me] = jnp.zeros((8, L), F32)
@@ -244,6 +272,7 @@
         w = w_out[:, j * L:(j + 1) * L]
         w_sq = w_sq + jnp.sum((w * w).reshape(HR // 8, 8, L), axis=0)
     m4[me, 2:3, :] = jnp.sum(w_sq, axis=0, keepdims=True)
+    m4_out = bcast(m4, m4_send, m4_recv)
 
     exchange_wait(m1, m1_send, m1_recv)
     b2 = beta[...]
@@ -295,14 +324,13 @@
         new, fr = row_factor(r_old[rows, :], rows, level[2], D)
         s = jnp.zeros((n, L), F32)
         for j in range(NB_OUT):
-            s = s + g2[rows, j * L:(j + 1) * L] * fac[5, j:j + 1, :]
+            s = s + g2_out[lo:lo + n, j * L:(j + 1) * L] * fac[5, j:j + 1, :]
         usq = usq + jnp.sum(s * (fr * fr), axis=0, keepdims=True)
         row_sq[rows, :] = fr
         r_old[rows, :] = new
     m3[me, 2:3, :] = usq
     m3[me, 3:4, :] = jnp.zeros((1, L), F32)
     m3_out = bcast(m3, m3_send, m3_recv)
-    m4_out = bcast(m4, m4_send, m4_recv)
 
     for b, ref in enumerate((acc, grecv)):
         fr = row_sq[b * L:(b + 1) * L, :]
@@ -336,6 +364,8 @@
 
     for i in range(NC):
         x_send(i).wait_send()
+    for p in range(HEAD):
+        hid_send(p).wait_send()
     for cp in m1_out + m2_out + m3_out + m4_out:
         cp.wait_send()
 
@@ -343,31 +373,33 @@
 def write_kernel(d_in, d_out, w_in, w_out, rin, cin, rout, cout, kappa,
                  wi_hbm, ri_hbm, ci_hbm, wo_hbm, ro_hbm, co_hbm, st_in, st_out, sem, sem_small):
     copies = []
+
+    def put(src, dst, s):
+        cp = pltpu.make_async_copy(src, dst, s)
+        cp.start()
+        copies.append(cp)
+
+    n = len(copies)
+    for lo, h in PARTS_OUT:
+        r = slice(lo, lo + h)
+        for j in range(NB_OUT):
+            c = slice(j * L, (j + 1) * L)
+            st_out[r, c] = w_out[r, c] - kappa[2:3, :] * d_out[r, c]
+        put(st_out.at[pl.ds(lo, h)], wo_hbm.at[pl.ds(lo, h)], sem.at[n])
+        n += 1
     for k in range(2):
-        kap = kappa[k:k + 1, :]
-        for h in range(4):
-            r = slice(h * 32, (h + 1) * 32)
+        for lo in range(0, XR, XR // 4):
+            h = XR // 4
+            r = slice(lo, lo + h)
             for j in range(NB_IN):
                 c = slice(j * L, (j + 1) * L)
-                st_in[k, r, c] = w_in[k, r, c] - kap * d_in[k, r, c]
-            cp = pltpu.make_async_copy(st_in.at[k, pl.ds(h * 32, 32)], wi_hbm.at[k, pl.ds(h * 32, 32)],
-                                       sem.at[4 * k + h])
-            cp.start()
-            copies.append(cp)
-    small = [pltpu.make_async_copy(a, b, sem_small.at[n]) for n, (a, b) in enumerate(
-        ((rin, ri_hbm), (cin, ci_hbm), (rout, ro_hbm), (cout, co_hbm)))]
-    for cp in small:
-        cp.start()
-    kap = kappa[2:3, :]
-    for h in range(4):
-        r = slice(h * 88, (h + 1) * 88)
-        for j in range(NB_OUT):
-            c = slice(j * L, (j + 1) * L)
-            st_out[r, c] = w_out[r, c] - kap * d_out[r, c]
-        cp = pltpu.make_async_copy(st_out.at[pl.ds(h * 88, 88)], wo_hbm.at[pl.ds(h * 88, 88)], sem.at[8 + h])
-        cp.start()
-        copies.append(cp)
-    for cp in copies + small:
+                st_in[k, r, c] = w_in[k, r, c] - kappa[k:k + 1, :] * d_in[k, r, c]
+            put(st_in.at[k, pl.ds(lo, h)], wi_hbm.at[k, pl.ds(lo, h)], sem.at[n])
+            n += 1
+        if k == 0:
+            for m, (a, b) in enumerate(((rin, ri_hbm), (cin, ci_hbm), (rout, ro_hbm), (cout, co_hbm))):
+                put(a, b, sem_small.at[m])
+    for cp in copies:
         cp.wait()
 
 
@@ -385,18 +417,20 @@
         scratch_shapes=[
             pltpu.VMEM((T, XR), jnp.bfloat16), pltpu.VMEM((T, XR), jnp.bfloat16),
             pltpu.VMEM((2 * XR, KC), jnp.bfloat16), pltpu.VMEM((2 * XR, KC), jnp.bfloat16),
-            pltpu.VMEM((HR, T), jnp.bfloat16), pltpu.VMEM((3, KC, FF), jnp.bfloat16),
-            pltpu.VMEM((2 * XR, FF), F32), pltpu.VMEM((XR, FF), F32), pltpu.VMEM((2 * L + 3 * L, FF), F32),
+            pltpu.VMEM((HR, T), jnp.bfloat16), pltpu.VMEM((SLOTS, KC, FF), jnp.bfloat16),
+            pltpu.VMEM((2 * XR, FF), F32), pltpu.VMEM((XR, FF), F32), pltpu.VMEM((2 * L, FF), F32), pltpu.VMEM((HR, D), F32),
+            pltpu.VMEM((HR, D), F32), pltpu.VMEM((HR, D), F32),
             pltpu.VMEM((ND, 32, L), F32), pltpu.VMEM((ND, 8, L), F32), pltpu.VMEM((ND, 4, L), F32),
             pltpu.VMEM((ND, 8, L), F32), pltpu.VMEM((5 * L, L), F32), pltpu.VMEM((5 * L, L), F32),
             pltpu.VMEM((6, NP, L), F32), pltpu.VMEM((3, NP, L), F32), pltpu.VMEM((1, 3 * L), F32),
             pltpu.VMEM((2, XR), F32), pltpu.VMEM((2, FF), F32), pltpu.VMEM((HR,), F32), pltpu.VMEM((1, D), F32),
             pltpu.VMEM((1, 1), F32), pltpu.VMEM((1, 1), F32), pltpu.VMEM((1, 1), F32), pltpu.VMEM((1, 1), F32),
-            dma(()), dma((len(PIECES),)), dma((len(PIECES),)), dma((NC,)), dma((2,)), dma((8,)), dma((NC,)), dma((NC,)),
+            dma(()), dma((PIECES,)), dma((PIECES,)), dma((NC,)), dma((2,)), dma((8,)), dma((NC,)), dma((NC,)),
+            dma((HEAD,)), dma((HEAD,)), dma((2,)),
             dma(()), dma(()), dma((ND,)), dma((ND,)), dma((ND,)), dma((ND,)), dma((ND,)), dma((ND,)), dma((ND,)),
             dma((ND,)),
         ],
-        compiler_params=pltpu.CompilerParams(collective_id=0, has_side_effects=True, vmem_limit_bytes=50 << 20),
+        compiler_params=pltpu.CompilerParams(collective_id=0, has_side_effects=True, vmem_limit_bytes=52 << 20),
         name="grad_stats",
     )(x_norm, hid_act.T, dy_in, dy_out, w_in, w_out, row_in, col_in,
       row_out, col_out.reshape(1, D),

time: 40.6 us -> 40.3 us (level)
  no operation moved by 1% of the time
where the time goes in v3:
time: 40.3 us; the launch traced here: 40.2 us
  Pallas kernels  36.8 us (91%)
  between operations  3.39 us (8%)
    pallas_call x1, Pallas kernels, local_step(): pl.pallas_call(grad_kernel, out_shape=[pltpu.VMEM(s, F32) for s in mids],...  34.6 us
    pallas_call x1, Pallas kernels, local_step(): pl.pallas_call(write_kernel, out_shape=[pltpu.HBM(s, F32) for s in outs],...  2.21 us

profile of v3, /device:TPU:0, one launch (start us, length us, event | category | flops | bytes accessed | tf_op | source)
XLA Modules:
  0.0 40.2 jit_solution(9354554788771715166)
XLA Ops:
  3.2 34.6 %grad_stats.1 = (f32[2,128,2816]{2,1,0:T(8,128)S(1)}, f32[352,1024]{1,0:T(8,128)S(1)}, f32[2,128,2816]{2,1,0:T(8,128)S(1)}, f32[352,1024]{1,0:T(8,128)S(1)}, f32...) custom-call(bf16[8192,128]{1,0:T(8,128)(2,1)} %x_hbm.1, ...), custom_call_target="tpu_custom_call" | custom-call | tf_op jit(solution)/shard_map/grad_stats/pallas_call | solution.py:412
  37.8 2.2 %write_weights.1 = (f32[2,128,2816]{2,1,0:T(8,128)}, f32[2,128]{1,0:T(2,128)}, f32[2,2816]{1,0:T(2,128)}, f32[352,1024]{1,0:T(8,128)}, f32[352]{0:T(512)}, /*index=5*/f32[1,1024]{1,0:T(1,128)}) custom-call(f32[2,128,2816]{2,1,0:T(8,128)S(1)} %get-tuple-element.21.d_in, f32[352,1024]{1,0:T(8,128)S(1)} %get-tuple-element.22.d_out, ...), custom_call_target="tpu_custom_call" | custom-call | tf_op jit(solution)/shard_map/write_weights/pallas_call | solution.py:440

commit v4 on v3

--- a/solution.py
+++ b/solution.py
@@ -96,11 +96,13 @@
             pltpu.make_async_remote_copy(buf.at[src], buf.at[src], send.at[k], recv.at[src],
                                          device_id=(src,), device_id_type=MESH).wait_recv()
 
+    x_loads = [pltpu.make_async_copy(x_hbm.at[r, :], x_own.at[r, :], s_x.at[n])
+               for n, r in enumerate((pl.ds(0, KC), pl.ds(KC, T - KC)))]
     start_out(0)
-    x_load = pltpu.make_async_copy(x_hbm, x_own, s_x)
-    x_load.start()
+    x_loads[0].start()
     start_out(1)
     dyi_copy(0).start()
+    x_loads[1].start()
     dyi_copy(1).start()
     small = [pltpu.make_async_copy(a, b, s_small.at[n]) for n, (a, b) in enumerate(
         ((ri_hbm, ri), (ci_hbm, ci), (ro_hbm, ro), (co_hbm, co),
@@ -128,12 +130,14 @@
             if n < len(extra):
                 extra[n]()
 
-    def partner_step(p):
+    def partner_step(p, turn=False):
         for n in range(D // TILE):
             c = pl.ds(n * TILE, TILE)
             v = jnp.dot(hid[:, pl.ds((HEAD + p) * KC, KC)], ring[0, :, pl.ds(p * D + n * TILE, TILE)],
                         preferred_element_type=F32)
             go_send[:, c] = v if p == 0 else go_send[:, c] + v
+            if turn:
+                transpose(1, n)
 
     xt = (xt0, xt1)
     QT = KC // 4
@@ -152,35 +156,40 @@
             c = slice(c0, c0 + TILE)
             v = jnp.dot(xt[i % 2][rows, :], ring[(i + 1) % SLOTS, :, c], preferred_element_type=F32)
             acc[rows, c] = v if i == 0 else acc[rows, c] + v
-            if n < 4 and i + 1 < NC:
+            if n < 4 and 0 < i < NC - 1:
                 transpose(i + 1, n)
 
     go_copy = pltpu.make_async_remote_copy(go_send, go_recv, go_sems.at[0], go_sems.at[1],
                                            device_id=(peer,), device_id_type=MESH)
     pl.semaphore_wait(barrier, ND - 1)
+    x_loads[0].wait()
+    x_send(0).start()
+    wait_out(0)
+    out_step(0)
+    dyi_copy(2).start()
     for p in range(HEAD):
         hid_send(p).start()
-    wait_out(0)
-    out_step(0)
-    x_load.wait()
-    for i in range(NC):
-        x_send(i).start()
-    dyi_copy(2).start()
     wait_out(1)
     out_step(1)
-    for p in range(HEAD):
-        hid_send(p).wait_recv()
-        partner_step(p)
-    dyi_copy(3).start()
     x_send(0).wait_recv()
     for n in range(4):
         transpose(0, n)
     for i in range(NC):
-        if i + 1 < NC:
+        if 0 < i < NC - 1:
             x_send(i + 1).wait_recv()
         dyi_copy(i).wait()
         in_step(i)
         if i == 0:
+            x_loads[1].wait()
+            for k in range(1, NC):
+                x_send(k).start()
+            hid_send(0).wait_recv()
+            partner_step(0)
+            hid_send(1).wait_recv()
+            x_send(1).wait_recv()
+            partner_step(1, True)
+            dyi_copy(3).start()
+        if i == 1:
             go_copy.start()
         if i in (1, 3):
             dyi_copy(i + 3).start()
@@ -425,7 +434,7 @@
             pltpu.VMEM((6, NP, L), F32), pltpu.VMEM((3, NP, L), F32), pltpu.VMEM((1, 3 * L), F32),
             pltpu.VMEM((2, XR), F32), pltpu.VMEM((2, FF), F32), pltpu.VMEM((HR,), F32), pltpu.VMEM((1, D), F32),
             pltpu.VMEM((1, 1), F32), pltpu.VMEM((1, 1), F32), pltpu.VMEM((1, 1), F32), pltpu.VMEM((1, 1), F32),
-            dma(()), dma((PIECES,)), dma((PIECES,)), dma((NC,)), dma((2,)), dma((8,)), dma((NC,)), dma((NC,)),
+            dma((2,)), dma((PIECES,)), dma((PIECES,)), dma((NC,)), dma((2,)), dma((8,)), dma((NC,)), dma((NC,)),
             dma((HEAD,)), dma((HEAD,)), dma((2,)),
             dma(()), dma(()), dma((ND,)), dma((ND,)), dma((ND,)), dma((ND,)), dma((ND,)), dma((ND,)), dma((ND,)),
             dma((ND,)),

time: 40.3 us -> 40 us (level)
  no operation moved by 1% of the time
where the time goes in v4:
time: 40 us; the launch traced here: 39.9 us
  Pallas kernels  36.5 us (91%)
  between operations  3.39 us (8%)
    pallas_call x1, Pallas kernels, local_step(): pl.pallas_call(grad_kernel, out_shape=[pltpu.VMEM(s, F32) for s in mids],...  34.3 us
    pallas_call x1, Pallas kernels, local_step(): pl.pallas_call(write_kernel, out_shape=[pltpu.HBM(s, F32) for s in outs],...  2.21 us

profile of v4, /device:TPU:0, one launch (start us, length us, event | category | flops | bytes accessed | tf_op | source)
XLA Modules:
  0.0 39.9 jit_solution(13525849442759513773)
XLA Ops:
  3.2 34.3 %grad_stats.1 = (f32[2,128,2816]{2,1,0:T(8,128)S(1)}, f32[352,1024]{1,0:T(8,128)S(1)}, f32[2,128,2816]{2,1,0:T(8,128)S(1)}, f32[352,1024]{1,0:T(8,128)S(1)}, f32...) custom-call(bf16[8192,128]{1,0:T(8,128)(2,1)} %x_hbm.1, ...), custom_call_target="tpu_custom_call" | custom-call | tf_op jit(solution)/shard_map/grad_stats/pallas_call | solution.py:421
  37.6 2.2 %write_weights.1 = (f32[2,128,2816]{2,1,0:T(8,128)}, f32[2,128]{1,0:T(2,128)}, f32[2,2816]{1,0:T(2,128)}, f32[352,1024]{1,0:T(8,128)}, f32[352]{0:T(512)}, /*index=5*/f32[1,1024]{1,0:T(1,128)}) custom-call(f32[2,128,2816]{2,1,0:T(8,128)S(1)} %get-tuple-element.21.d_in, f32[352,1024]{1,0:T(8,128)S(1)} %get-tuple-element.22.d_out, ...), custom_call_target="tpu_custom_call" | custom-call | tf_op jit(solution)/shard_map/write_weights/pallas_call | solution.py:449

commit v5 on v4

--- a/solution.py
+++ b/solution.py
@@ -41,7 +41,7 @@
 def grad_kernel(x_hbm, hid_hbm, dyi_hbm, dyo_hbm, wi_hbm, wo_hbm, ri_hbm, ci_hbm, ro_hbm, co_hbm,
                 beta_hbm, rel_hbm, crms_hbm, cnorm_hbm,
                 d_in, d_out, w_in, w_out, rin_new, cin_new, rout_new, cout_new, kappa,
-                x_own, x_peer, xt0, xt1, hid, ring, acc, grecv, g2, g2_out, go_send, go_recv, m1, m2, m3, m4, row_sq, r_old, fac, c_old, rpad,
+                x_own, x_peer, xt0, xt1, hid, ring, acc, grecv, go_send, go_recv, m1, m2, m3, m4, row_sq, r_old, fac, c_old, rpad,
                 ri, ci, ro, co, beta, rel, crms, cnorm,
                 s_x, s_hid, s_dyo, s_dyi, s_w, s_small, xs_send, xs_recv, hs_send, hs_recv, go_sems, g_send, g_recv,
                 m1_send, m1_recv, m2_send, m2_recv, m3_send, m3_recv, m4_send, m4_recv):
@@ -227,9 +227,7 @@
             for j in range(NB_IN):
                 c = slice(j * L, (j + 1) * L)
                 g = ref[0:XR, c]
-                g = g * g
-                g2[b * L:(b + 1) * L, c] = g
-                s = s + g
+                s = s + g * g
             row_sq[b * L:(b + 1) * L, :] = jnp.broadcast_to(jnp.sum(s, axis=1, keepdims=True), (XR, L))
         return body
 
@@ -261,9 +259,7 @@
         for j in range(NB_OUT):
             c = slice(j * L, (j + 1) * L)
             g = d_out[lo:lo + n, c]
-            g = g * g
-            g2_out[lo:lo + n, c] = g
-            s = s + g
+            s = s + g * g
         row_sq[2 * L + lo:2 * L + lo + n, :] = jnp.broadcast_to(jnp.sum(s, axis=1, keepdims=True), (n, L))
     g_copy.wait()
     stats_own(1, grecv)()
@@ -307,9 +303,7 @@
         nb = NP if k < 2 else NB_OUT
         new = b2 * c_old[k, 0:nb] + mix * (gs * (gs * col[k]) / shape[k][0] + EPS_ONE)
         c_old[k, 0:nb] = new
-        t = gs * lax.rsqrt(new)
-        fac[k, 0:nb] = t
-        fac[3 + k, 0:nb] = t * t
+        fac[k, 0:nb] = gs * lax.rsqrt(new)
 
     def row_factor(old, rows, lvl, n):
         new = b2 * old + mix * (gs * (gs * row_sq[rows, :]) / n + EPS_ONE)
@@ -317,13 +311,14 @@
 
     is0 = core == 0
     ks = (core, other)
-    for b in range(2):
+    for b, ref in enumerate((acc, grecv)):
         rows = slice(b * L, (b + 1) * L)
         lvl = jnp.where(is0 if b == 0 else jnp.logical_not(is0), level[0], level[1])
         new, fr = row_factor(r_old[pl.ds(pl.multiple_of(ks[b] * L, L), L), :], rows, lvl, FF)
         s = jnp.zeros((XR, L), F32)
         for j in range(NB_IN):
-            s = s + g2[rows, j * L:(j + 1) * L] * fac[3 + ks[b], j:j + 1, :]
+            v = ref[0:XR, j * L:(j + 1) * L] * fac[ks[b], j:j + 1, :]
+            s = s + v * v
         m3[me, pl.ds(ks[b], 1), :] = jnp.sum(s * (fr * fr), axis=0, keepdims=True)
         row_sq[rows, :] = fr
         r_old[pl.ds(pl.multiple_of(ks[b] * L, L), L), :] = new
@@ -333,7 +328,8 @@
         new, fr = row_factor(r_old[rows, :], rows, level[2], D)
         s = jnp.zeros((n, L), F32)
         for j in range(NB_OUT):
-            s = s + g2_out[lo:lo + n, j * L:(j + 1) * L] * fac[5, j:j + 1, :]
+            v = d_out[lo:lo + n, j * L:(j + 1) * L] * fac[2, j:j + 1, :]
+            s = s + v * v
         usq = usq + jnp.sum(s * (fr * fr), axis=0, keepdims=True)
         row_sq[rows, :] = fr
         r_old[rows, :] = new
@@ -427,11 +423,11 @@
             pltpu.VMEM((T, XR), jnp.bfloat16), pltpu.VMEM((T, XR), jnp.bfloat16),
             pltpu.VMEM((2 * XR, KC), jnp.bfloat16), pltpu.VMEM((2 * XR, KC), jnp.bfloat16),
             pltpu.VMEM((HR, T), jnp.bfloat16), pltpu.VMEM((SLOTS, KC, FF), jnp.bfloat16),
-            pltpu.VMEM((2 * XR, FF), F32), pltpu.VMEM((XR, FF), F32), pltpu.VMEM((2 * L, FF), F32), pltpu.VMEM((HR, D), F32),
+            pltpu.VMEM((2 * XR, FF), F32), pltpu.VMEM((XR, FF), F32),
             pltpu.VMEM((HR, D), F32), pltpu.VMEM((HR, D), F32),
             pltpu.VMEM((ND, 32, L), F32), pltpu.VMEM((ND, 8, L), F32), pltpu.VMEM((ND, 4, L), F32),
             pltpu.VMEM((ND, 8, L), F32), pltpu.VMEM((5 * L, L), F32), pltpu.VMEM((5 * L, L), F32),
-            pltpu.VMEM((6, NP, L), F32), pltpu.VMEM((3, NP, L), F32), pltpu.VMEM((1, 3 * L), F32),
+            pltpu.VMEM((3, NP, L), F32), pltpu.VMEM((3, NP, L), F32), pltpu.VMEM((1, 3 * L), F32),
             pltpu.VMEM((2, XR), F32), pltpu.VMEM((2, FF), F32), pltpu.VMEM((HR,), F32), pltpu.VMEM((1, D), F32),
             pltpu.VMEM((1, 1), F32), pltpu.VMEM((1, 1), F32), pltpu.VMEM((1, 1), F32), pltpu.VMEM((1, 1), F32),
             dma((2,)), dma((PIECES,)), dma((PIECES,)), dma((NC,)), dma((2,)), dma((8,)), dma((NC,)), dma((NC,)),

time: 40 us -> 40.2 us (level)
  no operation moved by 1% of the time
where the time goes in v5:
time: 40.2 us; the launch traced here: 40 us
  Pallas kernels  36.7 us (91%)
  between operations  3.39 us (8%)
    pallas_call x1, Pallas kernels, local_step(): pl.pallas_call(grad_kernel, out_shape=[pltpu.VMEM(s, F32) for s in mids],...  34.4 us
    pallas_call x1, Pallas kernels, local_step(): pl.pallas_call(write_kernel, out_shape=[pltpu.HBM(s, F32) for s in outs],...  2.21 us

profile of v5, /device:TPU:0, one launch (start us, length us, event | category | flops | bytes accessed | tf_op | source)
XLA Modules:
  0.0 40.0 jit_solution(9688691549890528095)
XLA Ops:
  3.2 34.4 %grad_stats.1 = (f32[2,128,2816]{2,1,0:T(8,128)S(1)}, f32[352,1024]{1,0:T(8,128)S(1)}, f32[2,128,2816]{2,1,0:T(8,128)S(1)}, f32[352,1024]{1,0:T(8,128)S(1)}, f32...) custom-call(bf16[8192,128]{1,0:T(8,128)(2,1)} %x_hbm.1, ...), custom_call_target="tpu_custom_call" | custom-call | tf_op jit(solution)/shard_map/grad_stats/pallas_call | solution.py:417
  37.7 2.2 %write_weights.1 = (f32[2,128,2816]{2,1,0:T(8,128)}, f32[2,128]{1,0:T(2,128)}, f32[2,2816]{1,0:T(2,128)}, f32[352,1024]{1,0:T(8,128)}, f32[352]{0:T(512)}, /*index=5*/f32[1,1024]{1,0:T(1,128)}) custom-call(f32[2,128,2816]{2,1,0:T(8,128)S(1)} %get-tuple-element.21.d_in, f32[352,1024]{1,0:T(8,128)S(1)} %get-tuple-element.22.d_out, ...), custom_call_target="tpu_custom_call" | custom-call | tf_op jit(solution)/shard_map/write_weights/pallas_call | solution.py:445
